TPU v7x, 32 devices: a whole 2x2x4 slice. The times are simulated.
32 devices in a mesh: task: 4 (over z), mp: 8 (over y, x, core).
Axes of the slice: x: 2, y: 2, z: 4, core: 2. Of those that a mesh axis runs over, the one named last changes fastest.
Arguments:
- deter: float32 [1024, 4096], P('task', 'mp'), may hold values from -3 to 3
- draws: int32 [4, 32, 1024], P(None, None, 'task'), may hold values from 0 to 31
- actions: int32 [4, 1024], P(None, 'task'), may hold values from 0 to 17
- horizons: int32 [64], replicated, may hold values from 5 to 30, as said below
- offsets: int32 [4, 4], replicated, may hold values from 0 to 3, as said below
- embed_stoch: bfloat16 [1024, 1024], replicated, may hold values from -1 to 1
- embed_act: bfloat16 [18, 1024], replicated, may hold values from -6 to 6
- gru_weight: bfloat16 [5120, 3, 4096], P(None, None, 'mp'), may hold values from -0.078125 to 0.078125
- prior_weight: bfloat16 [4096, 1024], replicated, may hold values from -0.09375 to 0.09375
- logit_weight: bfloat16 [1024, 1024], replicated, may hold values from -0.75 to 0.75
- head_weight: bfloat16 [1024, 2], replicated, may hold values from -0.375 to 0.375
Outputs:
- log_prob: float32 [4, 1024], P(None, 'task')
- reward: float32 [4, 1024], P(None, 'task')
- continuation: float32 [4, 1024], P(None, 'task')
- final_deter: float32 [1024, 4096], P('task', 'mp')
Inputs may be any that keep to these rules, and one draw needn't show every extreme that they name: `horizons`: rows of task k are home rows k * (16) up to (k + 1) * 16 - 1. `offsets`: the 4 numbers of one row are distinct.
All inputs are finite; a program needn't handle non-finite values.
Results may differ from a plain program's by a relative error of at most 0.0045.
Values may be sent and summed in bfloat16 or wider, within the bound.
A program may use at most 128 MiB of HBM per device.

v0:
```python
import jax
import jax.numpy as jnp
from jax import lax
from jax.sharding import PartitionSpec as P

HID = 1024
GROUPS = 32
CLASSES = 32
ACTS = 18
TASKS = 64
BLK_DEV = 4
STEPS = 4
WSTART = 16


def normed_rows(values):
    entries = values.shape[-1]
    average = jnp.sum(values, axis=-1, keepdims=True) / entries
    squares = jnp.sum(values * values, axis=-1, keepdims=True) / entries
    return (values - average) * lax.rsqrt(squares - average * average + 1e-05)


def product(rows_in, weight):
    return jnp.dot(rows_in, weight, preferred_element_type=jnp.float32)


def recurrence(deter, embedded, gate_weight, living, det_full):
    carried = deter
    rows_here, det_share = deter.shape
    lows = []
    for moment in range(STEPS):
        low = carried.astype(jnp.bfloat16)
        gathered = lax.all_gather(low, "mp", axis=1, tiled=True)
        lows.append(gathered)
        joined = jnp.concatenate([embedded[moment], gathered], axis=1)
        parts = [product(joined, gate_weight[part]) for part in range(3)]
        sums = sum((jnp.sum(part, axis=1) for part in parts))
        squares = sum((jnp.sum(part * part, axis=1) for part in parts))
        sums, squares = lax.psum(jnp.stack([sums, squares]), "mp")
        average = sums / (3 * det_full)
        inverse = lax.rsqrt(squares / (3 * det_full) - average * average + 1e-05)
        normed = [(part - average[:, None]) * inverse[:, None] for part in parts]
        reset_gate = jax.nn.sigmoid(normed[0])
        candidate = jnp.tanh(reset_gate * normed[1])
        update = jax.nn.sigmoid(normed[2] - 1.0)
        renewed = update * candidate + (1.0 - update) * carried
        carried = jnp.where(living[moment][:, None] > 0, renewed, carried)
    return (carried, lows)


def on_device(
    deter,
    draws,
    actions,
    horizons,
    offsets,
    embed_stoch,
    embed_act,
    gru_weight,
    prior_weight,
    logit_weight,
    head_weight,
):
    holders = lax.axis_size("task")
    device = lax.axis_index("task")
    shards = lax.axis_size("mp")
    shard_index = lax.axis_index("mp")
    rows_here, det_share = deter.shape
    block_rows = rows_here // BLK_DEV
    per_task = rows_here * holders // TASKS
    own_rows = rows_here // shards
    places = jnp.arange(holders, dtype=jnp.int32)
    classes = jnp.arange(CLASSES, dtype=jnp.int32)
    running = jnp.cumsum(offsets, axis=0) % holders
    packed = jnp.concatenate([draws, actions[:, None]], axis=1).astype(jnp.bfloat16)
    packed = lax.all_gather(packed, "task")
    packed = packed.reshape(holders, STEPS, GROUPS + 1, BLK_DEV, block_rows)
    at_slot = (device + running) % holders
    picked = places[:, None, None] == at_slot[None]
    packed = jnp.sum(
        jnp.where(picked[:, :, None, :, None], packed.astype(jnp.float32), 0.0), axis=0
    ).astype(jnp.int32)
    packed = packed.reshape(STEPS, GROUPS + 1, rows_here)
    draws_home = jnp.transpose(packed[:, :GROUPS], (0, 2, 1))
    hot = (draws_home[:, :, :, None] == classes).astype(jnp.bfloat16)
    hot = hot.reshape(STEPS * rows_here, GROUPS * CLASSES)
    action_hot = (
        packed[:, GROUPS].reshape(-1)[:, None] == jnp.arange(ACTS, dtype=jnp.int32)
    ).astype(jnp.bfloat16)
    embed_pre = product(hot, embed_stoch) + product(action_hot, embed_act)
    embedded = jax.nn.silu(normed_rows(embed_pre)).astype(jnp.bfloat16)
    embedded = embedded.reshape(STEPS, rows_here, HID)
    home_rows = device * rows_here + jnp.arange(rows_here, dtype=jnp.int32)
    task_ids = jnp.arange(TASKS, dtype=jnp.int32)
    horizon_rows = jnp.sum(
        jnp.where((home_rows // per_task)[:, None] == task_ids, horizons, 0), axis=1
    )
    alive = horizon_rows[None] > WSTART + jnp.arange(STEPS, dtype=jnp.int32)[:, None]
    living = alive.astype(jnp.float32)
    gate_weight = jnp.transpose(gru_weight, (1, 0, 2))
    carried, lows = recurrence(deter, embedded, gate_weight, living, det_share * shards)
    target = (device + running[-1]) % holders
    sending = places[:, None] == target[None, :]
    blocks = carried.reshape(BLK_DEV, block_rows, det_share)
    outgoing = jnp.where(sending[:, :, None, None], blocks[None], 0.0).astype(jnp.bfloat16)
    arrived = lax.all_to_all(
        outgoing.reshape(holders * BLK_DEV * block_rows, det_share),
        "task",
        split_axis=0,
        concat_axis=0,
        tiled=True,
    ).reshape(holders, BLK_DEV, block_rows, det_share)
    taking = places[:, None] == ((device - running[-1]) % holders)[None, :]
    final = jnp.sum(
        jnp.where(taking[:, :, None, None], arrived.astype(jnp.float32), 0.0), axis=0
    ).reshape(rows_here, det_share)

    def own(array, axis):
        return lax.dynamic_slice_in_dim(array, shard_index * own_rows, own_rows, axis)

    state_rows = jnp.concatenate([own(low, 0) for low in lows], axis=0)
    hidden = jax.nn.silu(normed_rows(product(state_rows, prior_weight))).astype(jnp.bfloat16)
    raw = product(hidden, logit_weight).reshape(STEPS * own_rows, GROUPS, CLASSES)
    exponent = jnp.exp(5.0 * jnp.tanh(raw / 5.0))
    own_hot = own(draws_home, 1).reshape(STEPS * own_rows, GROUPS)[:, :, None] == classes
    chosen = jnp.sum(jnp.where(own_hot, exponent, 0.0), axis=-1)
    chances = 0.99 * chosen / jnp.sum(exponent, axis=-1) + 0.01 / CLASSES
    log_prob = jnp.sum(jnp.log(chances), axis=-1)
    head_out = product(hidden, head_weight)
    results = jnp.stack([log_prob, head_out[:, 0], jax.nn.sigmoid(head_out[:, 1])])
    results = results.reshape(3, STEPS, own_rows) * own(living, 1)[None]
    spread = lax.all_gather(results, ("task", "mp"))
    spread = spread.reshape(holders, shards, 3, STEPS, own_rows)
    spread = jnp.transpose(spread, (0, 2, 3, 1, 4)).reshape(holders, 3, STEPS, BLK_DEV, block_rows)
    source = (device - running) % holders
    from_home = places[:, None, None] == source[None]
    outs = jnp.sum(jnp.where(from_home[:, None, :, :, None], spread, 0.0), axis=0)
    outs = outs.reshape(3, STEPS, rows_here)
    return (outs[0], outs[1], outs[2], final)


def solution(mesh):
    in_specs = (
        P("task", "mp"),
        P(None, None, "task"),
        P(None, "task"),
        P(),
        P(),
        P(),
        P(),
        P(None, None, "mp"),
        P(),
        P(),
        P(),
    )
    out_specs = (P(None, "task"), P(None, "task"), P(None, "task"), P("task", "mp"))
    return jax.shard_map(
        on_device, mesh=mesh, in_specs=in_specs, out_specs=out_specs, check_vma=False
    )
```

profile of v0, /device:TPU:0, one launch (start us, length us, event | category | flops | bytes accessed | tf_op | source)
XLA Modules:
  0.0 310.5 jit_solution(17363063580489032251)
XLA Ops:
  7.2 1.9 convert_element_type.50
  12.0 15.7 %all_gather.20 = bf16[4,4,33,256]{3,1,2,0:T(4,128)(2,1)S(1)} all-gather(bf16[1,4,33,256]{3,1,2,0:T(4,128)(2,1)S(1)} %pad_maximum_fusion.16), channel_id=1, replica_groups=mesh['task'=4,'mp'=8] {'task'}, dimensions={0}, use_global_device_ids=true | all-gather | bytes 337920 | tf_op jit(solution)/shard_map/all_gather | solution.py:76
  29.6 2.6 fusion
  36.5 4.2 %all-gather.5.cloned.1.call-done = bf16[256,4096]{1,0:T(8,128)(2,1)} async-done(((bf16[256,512]{1,0:T(8,128)(2,1)}), bf16[256,4096]{1,0:T(8,128)(2,1)}) %all-gather.5.cloned.1.call-update) | async-done | bytes 2097168 | tf_op jit(solution)/shard_map/all_gather | solution.py:33
  40.7 4.9 %fusion.59 = (f32[256]{0:T(256)S(1)}, f32[256]{0:T(256)S(1)}, f32[256,512]{1,0:T(8,128)S(1)}) fusion(bf16[3,5120,512]{2,1,0:T(8,128)(2,1)} %bitcast.126, bf16[256,4096]{1,0:T(8,128)(2,1)} %all-gather.5.cloned.1.call-done, bf16[256,1024]{1,0:T(8,128)(2,1)S(1)} %copy.60), kind=kOutput, calls=%fused_computation.170 | convolution fusion | flops 1347812864 | bytes 8390656 | tf_op jit(solution)/shard_map/dot_general | solution.py:24
  45.6 4.8 %fusion.58 = (f32[256]{0:T(256)S(1)}, f32[256]{0:T(256)S(1)}, f32[256,512]{1,0:T(8,128)}) fusion(bf16[3,5120,512]{2,1,0:T(8,128)(2,1)} %bitcast.127, bf16[256,4096]{1,0:T(8,128)(2,1)S(1)} %copy-done.5, bf16[256,1024]{1,0:T(8,128)(2,1)S(1)} %copy.60), kind=kOutput, calls=%fused_computation.169 | convolution fusion | flops 1347812864 | bytes 8390656 | tf_op jit(solution)/shard_map/dot_general | solution.py:24
  50.4 4.9 %fusion.60 = (f32[256]{0:T(256)S(1)}, f32[256]{0:T(256)S(1)}, f32[256,512]{1,0:T(8,128)}) fusion(bf16[3,5120,512]{2,1,0:T(8,128)(2,1)} %bitcast.128, bf16[256,4096]{1,0:T(8,128)(2,1)S(1)} %copy-done.5, bf16[256,1024]{1,0:T(8,128)(2,1)S(1)} %copy.60), kind=kOutput, calls=%fused_computation.171 | convolution fusion | flops 1347812864 | bytes 8390656 | tf_op jit(solution)/shard_map/dot_general | solution.py:24
  55.4 13.1 %psum.28 = f32[2,256]{1,0:T(2,128)S(1)} all-reduce(f32[2,256]{1,0:T(2,128)S(1)} %pad_maximum_fusion.17), channel_id=1, replica_groups=mesh['task'=4,'mp'=8] {'mp'}, use_global_device_ids=true, to_apply=%region_11.12 | all-reduce | flops 512 | bytes 4096 | tf_op jit(solution)/shard_map/psum | solution.py:39
  68.5 2.4 fusion.63
  71.3 27.8 %all-gather.7.cloned.1.call-done = bf16[256,4096]{1,0:T(8,128)(2,1)} async-done(((bf16[256,512]{1,0:T(8,128)(2,1)}), bf16[256,4096]{1,0:T(8,128)(2,1)}) %all-gather.7.cloned.1.call-update) | async-done | bytes 2097168 | tf_op jit(solution)/shard_map/all_gather | solution.py:33
  99.1 4.9 %fusion.56 = (f32[256]{0:T(256)S(1)}, f32[256]{0:T(256)S(1)}, f32[256,512]{1,0:T(8,128)S(1)}) fusion(bf16[3,5120,512]{2,1,0:T(8,128)(2,1)} %bitcast.129, bf16[256,4096]{1,0:T(8,128)(2,1)} %all-gather.7.cloned.1.call-done, bf16[256,1024]{1,0:T(8,128)(2,1)S(1)} %copy.61), kind=kOutput, calls=%fused_computation.167 | convolution fusion | flops 1347812864 | bytes 8390656 | tf_op jit(solution)/shard_map/dot_general | solution.py:24
  104.0 4.8 %fusion.55 = (f32[256]{0:T(256)S(1)}, f32[256]{0:T(256)S(1)}, f32[256,512]{1,0:T(8,128)}) fusion(bf16[3,5120,512]{2,1,0:T(8,128)(2,1)} %bitcast.130, bf16[256,4096]{1,0:T(8,128)(2,1)S(1)} %copy-done.6, bf16[256,1024]{1,0:T(8,128)(2,1)S(1)} %copy.61), kind=kOutput, calls=%fused_computation.166 | convolution fusion | flops 1347812864 | bytes 8390656 | tf_op jit(solution)/shard_map/dot_general | solution.py:24
  108.8 4.8 %fusion.57 = (f32[256]{0:T(256)S(1)}, f32[256]{0:T(256)S(1)}, f32[256,512]{1,0:T(8,128)}) fusion(bf16[3,5120,512]{2,1,0:T(8,128)(2,1)} %bitcast.131, bf16[256,4096]{1,0:T(8,128)(2,1)S(1)} %copy-done.6, bf16[256,1024]{1,0:T(8,128)(2,1)S(1)} %copy.61), kind=kOutput, calls=%fused_computation.168 | convolution fusion | flops 1347812864 | bytes 8390656 | tf_op jit(solution)/shard_map/dot_general | solution.py:24
  113.7 13.1 %psum.29 = f32[2,256]{1,0:T(2,128)S(1)} all-reduce(f32[2,256]{1,0:T(2,128)S(1)} %pad_maximum_fusion.18), channel_id=1, replica_groups=mesh['task'=4,'mp'=8] {'mp'}, use_global_device_ids=true, to_apply=%region_18.19 | all-reduce | flops 512 | bytes 4096 | tf_op jit(solution)/shard_map/psum | solution.py:39
  126.8 2.4 fusion.62
  129.4 28.0 %all-gather.9.cloned.1.call-done = bf16[256,4096]{1,0:T(8,128)(2,1)} async-done(((bf16[256,512]{1,0:T(8,128)(2,1)}), bf16[256,4096]{1,0:T(8,128)(2,1)}) %all-gather.9.cloned.1.call-update) | async-done | bytes 2097168 | tf_op jit(solution)/shard_map/all_gather | solution.py:33
  157.4 4.9 %fusion.53 = (f32[256]{0:T(256)S(1)}, f32[256]{0:T(256)S(1)}, f32[256,512]{1,0:T(8,128)S(1)}) fusion(bf16[3,5120,512]{2,1,0:T(8,128)(2,1)} %bitcast.132, bf16[256,4096]{1,0:T(8,128)(2,1)} %all-gather.9.cloned.1.call-done, bf16[256,1024]{1,0:T(8,128)(2,1)S(1)} %copy.62), kind=kOutput, calls=%fused_computation.164 | convolution fusion | flops 1347812864 | bytes 8390656 | tf_op jit(solution)/shard_map/dot_general | solution.py:24
  162.4 4.1 %fusion.52 = (f32[256]{0:T(256)S(1)}, f32[256]{0:T(256)S(1)}, f32[256,512]{1,0:T(8,128)S(1)}) fusion(bf16[3,5120,512]{2,1,0:T(8,128)(2,1)} %bitcast.133, bf16[256,4096]{1,0:T(8,128)(2,1)S(1)} %copy-done.7, bf16[256,1024]{1,0:T(8,128)(2,1)S(1)} %copy.62), kind=kOutput, calls=%fused_computation.163 | convolution fusion | flops 1347812864 | bytes 8390656 | tf_op jit(solution)/shard_map/dot_general | solution.py:24
  166.5 4.8 %fusion.54 = (f32[256]{0:T(256)S(1)}, f32[256]{0:T(256)S(1)}, f32[256,512]{1,0:T(8,128)}) fusion(bf16[3,5120,512]{2,1,0:T(8,128)(2,1)} %bitcast.134, bf16[256,4096]{1,0:T(8,128)(2,1)S(1)} %copy-done.7, bf16[256,1024]{1,0:T(8,128)(2,1)S(1)} %copy.62), kind=kOutput, calls=%fused_computation.165 | convolution fusion | flops 1347812864 | bytes 8390656 | tf_op jit(solution)/shard_map/dot_general | solution.py:24
  171.3 13.1 %psum.30 = f32[2,256]{1,0:T(2,128)S(1)} all-reduce(f32[2,256]{1,0:T(2,128)S(1)} %pad_maximum_fusion.19), channel_id=1, replica_groups=mesh['task'=4,'mp'=8] {'mp'}, use_global_device_ids=true, to_apply=%region_25.26 | all-reduce | flops 512 | bytes 4096 | tf_op jit(solution)/shard_map/psum | solution.py:39
  184.4 2.2 fusion.61
  188.7 1.7 constant_dynamic-slice_fusion.3
  192.0 22.9 %all-gather.11.cloned.1.call-done = bf16[256,4096]{1,0:T(8,128)(2,1)} async-done(((bf16[256,512]{1,0:T(8,128)(2,1)}), bf16[256,4096]{1,0:T(8,128)(2,1)}) %all-gather.11.cloned.1.call-update) | async-done | bytes 2097168 | tf_op jit(solution)/shard_map/all_gather | solution.py:33
  214.9 4.9 %fusion.49 = (f32[256]{0:T(256)S(1)}, f32[256]{0:T(256)S(1)}, f32[256,512]{1,0:T(8,128)S(1)}) fusion(bf16[3,5120,512]{2,1,0:T(8,128)(2,1)} %bitcast.135, bf16[256,4096]{1,0:T(8,128)(2,1)} %all-gather.11.cloned.1.call-done, bf16[256,1024]{1,0:T(8,128)(2,1)S(1)} %copy.67), kind=kOutput, calls=%fused_computation.160 | convolution fusion | flops 1347812864 | bytes 8390656 | tf_op jit(solution)/shard_map/dot_general | solution.py:24
  219.8 4.1 %fusion.48 = (f32[256]{0:T(256)S(1)}, f32[256]{0:T(256)S(1)}, f32[256,512]{1,0:T(8,128)S(1)}) fusion(bf16[3,5120,512]{2,1,0:T(8,128)(2,1)} %bitcast.136, bf16[256,4096]{1,0:T(8,128)(2,1)S(1)} %copy-done.8, bf16[256,1024]{1,0:T(8,128)(2,1)S(1)} %copy.67), kind=kOutput, calls=%fused_computation.159 | convolution fusion | flops 1347812864 | bytes 8390656 | tf_op jit(solution)/shard_map/dot_general | solution.py:24
  224.0 4.1 %fusion.50 = (f32[256]{0:T(256)S(1)}, f32[256]{0:T(256)S(1)}, f32[256,512]{1,0:T(8,128)S(1)}) fusion(bf16[3,5120,512]{2,1,0:T(8,128)(2,1)} %bitcast.137, bf16[256,4096]{1,0:T(8,128)(2,1)S(1)} %copy-done.8, bf16[256,1024]{1,0:T(8,128)(2,1)S(1)} %copy.67), kind=kOutput, calls=%fused_computation.161 | convolution fusion | flops 1347812864 | bytes 8390656 | tf_op jit(solution)/shard_map/dot_general | solution.py:24
  228.1 13.3 %psum.31 = f32[2,256]{1,0:T(2,128)S(1)} all-reduce(f32[2,256]{1,0:T(2,128)S(1)} %pad_maximum_fusion.20), channel_id=1, replica_groups=mesh['task'=4,'mp'=8] {'mp'}, use_global_device_ids=true, to_apply=%region_38.39 | all-reduce | flops 512 | bytes 4096 | tf_op jit(solution)/shard_map/psum | solution.py:39
  243.1 4.6 %all-to-all-start = ((bf16[4,256,512]{2,1,0:T(8,128)(2,1)}), bf16[4,256,512]{2,1,0:T(8,128)(2,1)S(1)}, u32[]{:S(2)}, u32[]{:S(2)}) async-start(bf16[4,256,512]{2,1,0:T(8,128)(2,1)} %select_convert_fusion), calls=%async_computation | async-start | bytes 2097152 | tf_op jit(solution)/shard_map/all_to_all | solution.py:106
  248.7 5.1 %fusion.51 = (f32[128]{0:T(128)S(1)}, f32[128]{0:T(128)S(1)}, f32[128,1024]{1,0:T(8,128)S(1)}) fusion(bf16[4096,1024]{1,0:T(8,128)(2,1)} %param.19, bf16[32,4096]{1,0:T(8,128)(2,1)S(1)} %constant_dynamic-slice_fusion.1, bf16[32,4096]{1,0:T(8,128)(2,1)} %constant_dynamic-slice_fusion.2, bf16[32,4096]{1,0:T(8,128)(2,1)} %constant_dynamic-slice_fusion.3, ...), kind=kOutput, calls=%fused_computation.162 | convolution fusion | flops 1078329088 | bytes 9962496 | tf_op jit(solution)/shard_map/dot_general | solution.py:24
  254.5 2.9 fusion.17
  257.3 2.1 copy.63
  260.8 40.0 %all_gather.25 = f32[32,3,4,32]{3,2,1,0:T(4,128)S(1)} all-gather(f32[1,3,4,32]{3,2,1,0:T(4,128)S(1)} %maximum_multiply_fusion), channel_id=1, replica_groups=mesh['task'=4,'mp'=8] {'task','mp'}, dimensions={0}, use_global_device_ids=true | all-gather | bytes 50688 | tf_op jit(solution)/shard_map/all_gather | solution.py:132
  (120 shorter events, 21.3 us)
Async XLA Ops:
  7.2 22.4 %copy-start = (bf16[1024,1024]{1,0:T(8,128)(2,1)S(1)}, bf16[1024,1024]{1,0:T(8,128)(2,1)}, u32[]{:S(2)}) copy-start(bf16[1024,1024]{1,0:T(8,128)(2,1)} %param.16) | copy-start | bytes 6291460
  7.2 33.5 %all-gather.5.cloned.1.call-start = ((), (), s32[]{:S(2)}) async-start(), calls=%async_computation.1 | async-start | bytes 2359296 | tf_op jit(solution)/shard_map/all_gather | solution.py:33
  9.2 89.9 %all-gather.7.cloned.1.call-start = ((), (), s32[]{:S(2)}) async-start(), calls=%async_computation.2 | async-start | bytes 2359296 | tf_op jit(solution)/shard_map/all_gather | solution.py:33
  29.6 2.6 copy-start.4
  35.1 1.2 copy-start.10
  40.7 4.9 %copy-start.5 = (bf16[256,4096]{1,0:T(8,128)(2,1)S(1)}, bf16[256,4096]{1,0:T(8,128)(2,1)}, u32[]{:S(2)}) copy-start(bf16[256,4096]{1,0:T(8,128)(2,1)} %all-gather.5.cloned.1.call-done) | copy-start | bytes 6291460
  50.4 18.0 %copy-start.2 = (f32[256,512]{1,0:T(8,128)S(1)}, f32[256,512]{1,0:T(8,128)}, u32[]{:S(2)}) copy-start(f32[256,512]{1,0:T(8,128)} %param.11) | copy-start | bytes 1572868
  50.4 20.7 %copy-start.3 = (bf16[256,1024]{0,1:T(8,128)(2,1)S(1)}, bf16[256,1024]{0,1:T(8,128)(2,1)}, u32[]{:S(2)}) copy-start(bf16[256,1024]{0,1:T(8,128)(2,1)} %get-tuple-element.50) | copy-start | bytes 1572868
  70.9 86.6 %all-gather.9.cloned.1.call-start = ((), (), s32[]{:S(2)}) async-start(), calls=%async_computation.3 | async-start | bytes 2359296 | tf_op jit(solution)/shard_map/all_gather | solution.py:33
  99.1 4.9 %copy-start.6 = (bf16[256,4096]{1,0:T(8,128)(2,1)S(1)}, bf16[256,4096]{1,0:T(8,128)(2,1)}, u32[]{:S(2)}) copy-start(bf16[256,4096]{1,0:T(8,128)(2,1)} %all-gather.7.cloned.1.call-done) | copy-start | bytes 6291460
  129.2 85.7 %all-gather.11.cloned.1.call-start = ((), (), s32[]{:S(2)}) async-start(), calls=%async_computation.4 | async-start | bytes 2359296 | tf_op jit(solution)/shard_map/all_gather | solution.py:33
  157.4 4.9 %copy-start.7 = (bf16[256,4096]{1,0:T(8,128)(2,1)S(1)}, bf16[256,4096]{1,0:T(8,128)(2,1)}, u32[]{:S(2)}) copy-start(bf16[256,4096]{1,0:T(8,128)(2,1)} %all-gather.9.cloned.1.call-done) | copy-start | bytes 6291460
  214.9 4.9 %copy-start.8 = (bf16[256,4096]{1,0:T(8,128)(2,1)S(1)}, bf16[256,4096]{1,0:T(8,128)(2,1)}, u32[]{:S(2)}) copy-start(bf16[256,4096]{1,0:T(8,128)(2,1)} %all-gather.11.cloned.1.call-done) | copy-start | bytes 6291460
  243.1 59.8 %all-to-all-start = ((bf16[4,256,512]{2,1,0:T(8,128)(2,1)}), bf16[4,256,512]{2,1,0:T(8,128)(2,1)S(1)}, u32[]{:S(2)}, u32[]{:S(2)}) async-start(bf16[4,256,512]{2,1,0:T(8,128)(2,1)} %select_convert_fusion), calls=%async_computation | async-start | bytes 2097152 | tf_op jit(solution)/shard_map/all_to_all | solution.py:106
  248.7 5.4 %copy-start.9 = (bf16[1024,2]{0,1:T(2,128)(2,1)S(1)}, bf16[1024,2]{0,1:T(2,128)(2,1)}, u32[]{:S(2)}) copy-start(bf16[1024,2]{0,1:T(2,128)(2,1)} %param.21) | copy-start | bytes 12292
  248.7 55.3 %copy-start.1 = (bf16[1024,1024]{1,0:T(8,128)(2,1)S(1)}, bf16[1024,1024]{1,0:T(8,128)(2,1)}, u32[]{:S(2)}) copy-start(bf16[1024,1024]{1,0:T(8,128)(2,1)} %param.16) | copy-start | bytes 6291460
Sparse Core Ops, SparseCore 0:
  9.9 30.8 all-gather.4
  71.0 28.0 all-gather.6
  129.3 28.0 all-gather.8
  186.8 28.0 all-gather.10
where the time goes:
time: 312 us; the launch traced here: 311 us
  blocking collectives  108 us (35%)
  waiting for transfers between devices  83 us (27%)
  matrix products  68.2 us (22%)
  other arithmetic  17.7 us (6%)
  local copies, waits for them, and re-layouts  14.2 us (5%)
  between operations  14.2 us (5%)
  starting transfers between devices  4.94 us (2%)
    all_gather x4, waiting for transfers between devices, recurrence(): gathered = lax.all_gather(low, 'mp', axis=1, tiled=True)  83 us
    dot_general x17, matrix products, product(): return jnp.dot(rows_in, weight, preferred_element_type=jnp.float32)  68.2 us
    psum x4, blocking collectives, recurrence(): sums, squares = lax.psum(jnp.stack([sums, squares]), 'mp')  52.6 us
    all_gather x1, blocking collectives, on_device(): spread = lax.all_gather(results, ('task', 'mp'))  40 us
    all_gather x1, blocking collectives, on_device(): packed = lax.all_gather(packed, 'task')  15.7 us
    convert_element_type x4, other arithmetic, recurrence(): low = carried.astype(jnp.bfloat16)  8.9 us
  transfers between devices with their start and end apart: 5, of which 4 were waited for; matrix products, arithmetic and copies ran while one was open for 10% of the time, Pallas kernels for 0%

commit v1 on v0

--- a/solution.py
+++ b/solution.py
@@ -36,7 +36,7 @@
         parts = [product(joined, gate_weight[part]) for part in range(3)]
         sums = sum((jnp.sum(part, axis=1) for part in parts))
         squares = sum((jnp.sum(part * part, axis=1) for part in parts))
-        sums, squares = lax.psum(jnp.stack([sums, squares]), "mp")
+        sums, squares = jnp.sum(lax.all_gather(jnp.stack([sums, squares]), "mp"), axis=0)
         average = sums / (3 * det_full)
         inverse = lax.rsqrt(squares / (3 * det_full) - average * average + 1e-05)
         normed = [(part - average[:, None]) * inverse[:, None] for part in parts]

time: 312 us -> 296 us (0.949)
  blocking collectives: 108 us -> 93.1 us
    psum x4 -> x0, blocking collectives: 52.6 us -> none  [recurrence(): sums, squares = lax.psum(jnp.stack([sums, squares]), 'mp')]
    all_gather x0 -> x4, blocking collectives: none -> 35.7 us  [recurrence(): lax.all_gather(jnp.stack([sums, squares]), 'mp')]
  transfers between devices with their start and end apart: 5 -> 5, of which waited for: 4 -> 4; matrix products, arithmetic and copies ran while one was open for 10% -> 11% of each run, Pallas kernels for 0% -> 0%
where the time goes in v1:
time: 296 us; the launch traced here: 295 us
  blocking collectives  93.1 us (31%)
  waiting for transfers between devices  83 us (28%)
  matrix products  68.2 us (23%)
  other arithmetic  17.8 us (6%)
  local copies, waits for them, and re-layouts  14.2 us (5%)
  between operations  14.2 us (5%)
  starting transfers between devices  4.94 us (2%)
    all_gather x4, waiting for transfers between devices, recurrence(): gathered = lax.all_gather(low, 'mp', axis=1, tiled=True)  82.9 us
    dot_general x17, matrix products, product(): return jnp.dot(rows_in, weight, preferred_element_type=jnp.float32)  68.2 us
    all_gather x1, blocking collectives, on_device(): spread = lax.all_gather(results, ('task', 'mp'))  41.7 us
    all_gather x4, blocking collectives, recurrence(): lax.all_gather(jnp.stack([sums, squares]), 'mp')  35.7 us
    all_gather x1, blocking collectives, on_device(): packed = lax.all_gather(packed, 'task')  15.7 us
    convert_element_type x4, other arithmetic, recurrence(): low = carried.astype(jnp.bfloat16)  8.9 us
  transfers between devices with their start and end apart: 5, of which 4 were waited for; matrix products, arithmetic and copies ran while one was open for 11% of the time, Pallas kernels for 0%

profile of v1, /device:TPU:0, one launch (start us, length us, event | category | flops | bytes accessed | tf_op | source)
XLA Modules:
  0.0 295.4 jit_solution(3904869448127259675)
XLA Ops:
  7.2 1.9 convert_element_type.50
  12.0 15.7 %all_gather.44 = bf16[4,4,33,256]{3,1,2,0:T(4,128)(2,1)S(1)} all-gather(bf16[1,4,33,256]{3,1,2,0:T(4,128)(2,1)S(1)} %pad_maximum_fusion.16), channel_id=1, replica_groups=mesh['task'=4,'mp'=8] {'task'}, dimensions={0}, use_global_device_ids=true | all-gather | bytes 337920 | tf_op jit(solution)/shard_map/all_gather | solution.py:76
  29.6 2.6 fusion
  36.5 4.2 %all-gather.13.cloned.1.call-done = bf16[256,4096]{1,0:T(8,128)(2,1)} async-done(((bf16[256,512]{1,0:T(8,128)(2,1)}), bf16[256,4096]{1,0:T(8,128)(2,1)}) %all-gather.13.cloned.1.call-update) | async-done | bytes 2097168 | tf_op jit(solution)/shard_map/all_gather | solution.py:33
  40.7 4.9 %fusion.59 = (f32[256]{0:T(256)S(1)}, f32[256]{0:T(256)S(1)}, f32[256,512]{1,0:T(8,128)S(1)}) fusion(bf16[3,5120,512]{2,1,0:T(8,128)(2,1)} %bitcast.134, bf16[256,4096]{1,0:T(8,128)(2,1)} %all-gather.13.cloned.1.call-done, bf16[256,1024]{1,0:T(8,128)(2,1)S(1)} %copy.60), kind=kOutput, calls=%fused_computation.170 | convolution fusion | flops 1347812864 | bytes 8390656 | tf_op jit(solution)/shard_map/dot_general | solution.py:24
  45.6 4.8 %fusion.58 = (f32[256]{0:T(256)S(1)}, f32[256]{0:T(256)S(1)}, f32[256,512]{1,0:T(8,128)}) fusion(bf16[3,5120,512]{2,1,0:T(8,128)(2,1)} %bitcast.135, bf16[256,4096]{1,0:T(8,128)(2,1)S(1)} %copy-done.5, bf16[256,1024]{1,0:T(8,128)(2,1)S(1)} %copy.60), kind=kOutput, calls=%fused_computation.169 | convolution fusion | flops 1347812864 | bytes 8390656 | tf_op jit(solution)/shard_map/dot_general | solution.py:24
  50.4 4.9 %fusion.60 = (f32[256]{0:T(256)S(1)}, f32[256]{0:T(256)S(1)}, f32[256,512]{1,0:T(8,128)}) fusion(bf16[3,5120,512]{2,1,0:T(8,128)(2,1)} %bitcast.136, bf16[256,4096]{1,0:T(8,128)(2,1)S(1)} %copy-done.5, bf16[256,1024]{1,0:T(8,128)(2,1)S(1)} %copy.60), kind=kOutput, calls=%fused_computation.171 | convolution fusion | flops 1347812864 | bytes 8390656 | tf_op jit(solution)/shard_map/dot_general | solution.py:24
  55.4 8.9 %all-gather.4 = f32[8,2,256]{2,1,0:T(2,128)S(1)} all-gather(f32[1,2,256]{2,1,0:T(2,128)S(1)} %maximum_bitcast_fusion), channel_id=2, replica_groups=mesh['task'=4,'mp'=8] {'mp'}, dimensions={0}, use_global_device_ids=true | all-gather | bytes 18432 | tf_op jit(solution)/shard_map/all_gather | solution.py:39
  64.3 2.4 fusion.63
  67.1 27.8 %all-gather.15.cloned.1.call-done = bf16[256,4096]{1,0:T(8,128)(2,1)} async-done(((bf16[256,512]{1,0:T(8,128)(2,1)}), bf16[256,4096]{1,0:T(8,128)(2,1)}) %all-gather.15.cloned.1.call-update) | async-done | bytes 2097168 | tf_op jit(solution)/shard_map/all_gather | solution.py:33
  94.9 4.9 %fusion.56 = (f32[256]{0:T(256)S(1)}, f32[256]{0:T(256)S(1)}, f32[256,512]{1,0:T(8,128)S(1)}) fusion(bf16[3,5120,512]{2,1,0:T(8,128)(2,1)} %bitcast.137, bf16[256,4096]{1,0:T(8,128)(2,1)} %all-gather.15.cloned.1.call-done, bf16[256,1024]{1,0:T(8,128)(2,1)S(1)} %copy.61), kind=kOutput, calls=%fused_computation.167 | convolution fusion | flops 1347812864 | bytes 8390656 | tf_op jit(solution)/shard_map/dot_general | solution.py:24
  99.8 4.8 %fusion.55 = (f32[256]{0:T(256)S(1)}, f32[256]{0:T(256)S(1)}, f32[256,512]{1,0:T(8,128)}) fusion(bf16[3,5120,512]{2,1,0:T(8,128)(2,1)} %bitcast.138, bf16[256,4096]{1,0:T(8,128)(2,1)S(1)} %copy-done.6, bf16[256,1024]{1,0:T(8,128)(2,1)S(1)} %copy.61), kind=kOutput, calls=%fused_computation.166 | convolution fusion | flops 1347812864 | bytes 8390656 | tf_op jit(solution)/shard_map/dot_general | solution.py:24
  104.6 4.8 %fusion.57 = (f32[256]{0:T(256)S(1)}, f32[256]{0:T(256)S(1)}, f32[256,512]{1,0:T(8,128)}) fusion(bf16[3,5120,512]{2,1,0:T(8,128)(2,1)} %bitcast.139, bf16[256,4096]{1,0:T(8,128)(2,1)S(1)} %copy-done.6, bf16[256,1024]{1,0:T(8,128)(2,1)S(1)} %copy.61), kind=kOutput, calls=%fused_computation.168 | convolution fusion | flops 1347812864 | bytes 8390656 | tf_op jit(solution)/shard_map/dot_general | solution.py:24
  109.5 8.9 %all-gather.5 = f32[8,2,256]{2,1,0:T(2,128)S(1)} all-gather(f32[1,2,256]{2,1,0:T(2,128)S(1)} %maximum_bitcast_fusion.1), channel_id=3, replica_groups=mesh['task'=4,'mp'=8] {'mp'}, dimensions={0}, use_global_device_ids=true | all-gather | bytes 18432 | tf_op jit(solution)/shard_map/all_gather | solution.py:39
  118.4 2.4 fusion.62
  121.0 28.0 %all-gather.17.cloned.1.call-done = bf16[256,4096]{1,0:T(8,128)(2,1)} async-done(((bf16[256,512]{1,0:T(8,128)(2,1)}), bf16[256,4096]{1,0:T(8,128)(2,1)}) %all-gather.17.cloned.1.call-update) | async-done | bytes 2097168 | tf_op jit(solution)/shard_map/all_gather | solution.py:33
  149.0 4.9 %fusion.53 = (f32[256]{0:T(256)S(1)}, f32[256]{0:T(256)S(1)}, f32[256,512]{1,0:T(8,128)S(1)}) fusion(bf16[3,5120,512]{2,1,0:T(8,128)(2,1)} %bitcast.140, bf16[256,4096]{1,0:T(8,128)(2,1)} %all-gather.17.cloned.1.call-done, bf16[256,1024]{1,0:T(8,128)(2,1)S(1)} %copy.62), kind=kOutput, calls=%fused_computation.164 | convolution fusion | flops 1347812864 | bytes 8390656 | tf_op jit(solution)/shard_map/dot_general | solution.py:24
  153.9 4.1 %fusion.52 = (f32[256]{0:T(256)S(1)}, f32[256]{0:T(256)S(1)}, f32[256,512]{1,0:T(8,128)S(1)}) fusion(bf16[3,5120,512]{2,1,0:T(8,128)(2,1)} %bitcast.141, bf16[256,4096]{1,0:T(8,128)(2,1)S(1)} %copy-done.7, bf16[256,1024]{1,0:T(8,128)(2,1)S(1)} %copy.62), kind=kOutput, calls=%fused_computation.163 | convolution fusion | flops 1347812864 | bytes 8390656 | tf_op jit(solution)/shard_map/dot_general | solution.py:24
  158.1 4.8 %fusion.54 = (f32[256]{0:T(256)S(1)}, f32[256]{0:T(256)S(1)}, f32[256,512]{1,0:T(8,128)}) fusion(bf16[3,5120,512]{2,1,0:T(8,128)(2,1)} %bitcast.142, bf16[256,4096]{1,0:T(8,128)(2,1)S(1)} %copy-done.7, bf16[256,1024]{1,0:T(8,128)(2,1)S(1)} %copy.62), kind=kOutput, calls=%fused_computation.165 | convolution fusion | flops 1347812864 | bytes 8390656 | tf_op jit(solution)/shard_map/dot_general | solution.py:24
  162.9 8.9 %all-gather.6 = f32[8,2,256]{2,1,0:T(2,128)S(1)} all-gather(f32[1,2,256]{2,1,0:T(2,128)S(1)} %maximum_bitcast_fusion.2), channel_id=4, replica_groups=mesh['task'=4,'mp'=8] {'mp'}, dimensions={0}, use_global_device_ids=true | all-gather | bytes 18432 | tf_op jit(solution)/shard_map/all_gather | solution.py:39
  171.8 2.2 fusion.61
  176.0 1.7 constant_dynamic-slice_fusion.3
  179.4 22.9 %all-gather.19.cloned.1.call-done = bf16[256,4096]{1,0:T(8,128)(2,1)} async-done(((bf16[256,512]{1,0:T(8,128)(2,1)}), bf16[256,4096]{1,0:T(8,128)(2,1)}) %all-gather.19.cloned.1.call-update) | async-done | bytes 2097168 | tf_op jit(solution)/shard_map/all_gather | solution.py:33
  202.3 4.9 %fusion.49 = (f32[256]{0:T(256)S(1)}, f32[256]{0:T(256)S(1)}, f32[256,512]{1,0:T(8,128)S(1)}) fusion(bf16[3,5120,512]{2,1,0:T(8,128)(2,1)} %bitcast.143, bf16[256,4096]{1,0:T(8,128)(2,1)} %all-gather.19.cloned.1.call-done, bf16[256,1024]{1,0:T(8,128)(2,1)S(1)} %copy.67), kind=kOutput, calls=%fused_computation.160 | convolution fusion | flops 1347812864 | bytes 8390656 | tf_op jit(solution)/shard_map/dot_general | solution.py:24
  207.2 4.1 %fusion.48 = (f32[256]{0:T(256)S(1)}, f32[256]{0:T(256)S(1)}, f32[256,512]{1,0:T(8,128)S(1)}) fusion(bf16[3,5120,512]{2,1,0:T(8,128)(2,1)} %bitcast.144, bf16[256,4096]{1,0:T(8,128)(2,1)S(1)} %copy-done.8, bf16[256,1024]{1,0:T(8,128)(2,1)S(1)} %copy.67), kind=kOutput, calls=%fused_computation.159 | convolution fusion | flops 1347812864 | bytes 8390656 | tf_op jit(solution)/shard_map/dot_general | solution.py:24
  211.3 4.1 %fusion.50 = (f32[256]{0:T(256)S(1)}, f32[256]{0:T(256)S(1)}, f32[256,512]{1,0:T(8,128)S(1)}) fusion(bf16[3,5120,512]{2,1,0:T(8,128)(2,1)} %bitcast.145, bf16[256,4096]{1,0:T(8,128)(2,1)S(1)} %copy-done.8, bf16[256,1024]{1,0:T(8,128)(2,1)S(1)} %copy.67), kind=kOutput, calls=%fused_computation.161 | convolution fusion | flops 1347812864 | bytes 8390656 | tf_op jit(solution)/shard_map/dot_general | solution.py:24
  215.5 9.1 %all-gather.7 = f32[8,2,256]{2,1,0:T(2,128)S(1)} all-gather(f32[1,2,256]{2,1,0:T(2,128)S(1)} %maximum_bitcast_fusion.3), channel_id=5, replica_groups=mesh['task'=4,'mp'=8] {'mp'}, dimensions={0}, use_global_device_ids=true | all-gather | bytes 18432 | tf_op jit(solution)/shard_map/all_gather | solution.py:39
  226.3 4.6 %all-to-all-start = ((bf16[4,256,512]{2,1,0:T(8,128)(2,1)}), bf16[4,256,512]{2,1,0:T(8,128)(2,1)S(1)}, u32[]{:S(2)}, u32[]{:S(2)}) async-start(bf16[4,256,512]{2,1,0:T(8,128)(2,1)} %select_convert_fusion), calls=%async_computation | async-start | bytes 2097152 | tf_op jit(solution)/shard_map/all_to_all | solution.py:106
  231.9 5.0 %fusion.51 = (f32[128]{0:T(128)S(1)}, f32[128]{0:T(128)S(1)}, f32[128,1024]{1,0:T(8,128)S(1)}) fusion(bf16[4096,1024]{1,0:T(8,128)(2,1)} %param.19, bf16[32,4096]{1,0:T(8,128)(2,1)S(1)} %constant_dynamic-slice_fusion.1, bf16[32,4096]{1,0:T(8,128)(2,1)} %constant_dynamic-slice_fusion.2, bf16[32,4096]{1,0:T(8,128)(2,1)} %constant_dynamic-slice_fusion.3, ...), kind=kOutput, calls=%fused_computation.162 | convolution fusion | flops 1078329088 | bytes 9962496 | tf_op jit(solution)/shard_map/dot_general | solution.py:24
  237.6 2.9 fusion.17
  240.5 2.1 copy.63
  244.0 41.7 %all_gather.55 = f32[32,3,4,32]{3,2,1,0:T(4,128)S(1)} all-gather(f32[1,3,4,32]{3,2,1,0:T(4,128)S(1)} %maximum_multiply_fusion), channel_id=1, replica_groups=mesh['task'=4,'mp'=8] {'task','mp'}, dimensions={0}, use_global_device_ids=true | all-gather | bytes 50688 | tf_op jit(solution)/shard_map/all_gather | solution.py:132
  (124 shorter events, 21.4 us)
Async XLA Ops:
  7.2 22.4 %copy-start = (bf16[1024,1024]{1,0:T(8,128)(2,1)S(1)}, bf16[1024,1024]{1,0:T(8,128)(2,1)}, u32[]{:S(2)}) copy-start(bf16[1024,1024]{1,0:T(8,128)(2,1)} %param.16) | copy-start | bytes 6291460
  7.2 33.5 %all-gather.13.cloned.1.call-start = ((), (), s32[]{:S(2)}) async-start(), calls=%async_computation.1 | async-start | bytes 2359296 | tf_op jit(solution)/shard_map/all_gather | solution.py:33
  9.2 85.7 %all-gather.15.cloned.1.call-start = ((), (), s32[]{:S(2)}) async-start(), calls=%async_computation.2 | async-start | bytes 2359296 | tf_op jit(solution)/shard_map/all_gather | solution.py:33
  29.6 2.6 copy-start.4
  35.1 1.2 copy-start.10
  40.7 4.9 %copy-start.5 = (bf16[256,4096]{1,0:T(8,128)(2,1)S(1)}, bf16[256,4096]{1,0:T(8,128)(2,1)}, u32[]{:S(2)}) copy-start(bf16[256,4096]{1,0:T(8,128)(2,1)} %all-gather.13.cloned.1.call-done) | copy-start | bytes 6291460
  50.4 13.8 %copy-start.2 = (f32[256,512]{1,0:T(8,128)S(1)}, f32[256,512]{1,0:T(8,128)}, u32[]{:S(2)}) copy-start(f32[256,512]{1,0:T(8,128)} %param.11) | copy-start | bytes 1572868
  50.4 16.5 %copy-start.3 = (bf16[256,1024]{0,1:T(8,128)(2,1)S(1)}, bf16[256,1024]{0,1:T(8,128)(2,1)}, u32[]{:S(2)}) copy-start(bf16[256,1024]{0,1:T(8,128)(2,1)} %get-tuple-element.50) | copy-start | bytes 1572868
  66.7 82.3 %all-gather.17.cloned.1.call-start = ((), (), s32[]{:S(2)}) async-start(), calls=%async_computation.3 | async-start | bytes 2359296 | tf_op jit(solution)/shard_map/all_gather | solution.py:33
  94.9 4.9 %copy-start.6 = (bf16[256,4096]{1,0:T(8,128)(2,1)S(1)}, bf16[256,4096]{1,0:T(8,128)(2,1)}, u32[]{:S(2)}) copy-start(bf16[256,4096]{1,0:T(8,128)(2,1)} %all-gather.15.cloned.1.call-done) | copy-start | bytes 6291460
  120.8 81.5 %all-gather.19.cloned.1.call-start = ((), (), s32[]{:S(2)}) async-start(), calls=%async_computation.4 | async-start | bytes 2359296 | tf_op jit(solution)/shard_map/all_gather | solution.py:33
  149.0 4.9 %copy-start.7 = (bf16[256,4096]{1,0:T(8,128)(2,1)S(1)}, bf16[256,4096]{1,0:T(8,128)(2,1)}, u32[]{:S(2)}) copy-start(bf16[256,4096]{1,0:T(8,128)(2,1)} %all-gather.17.cloned.1.call-done) | copy-start | bytes 6291460
  202.3 4.9 %copy-start.8 = (bf16[256,4096]{1,0:T(8,128)(2,1)S(1)}, bf16[256,4096]{1,0:T(8,128)(2,1)}, u32[]{:S(2)}) copy-start(bf16[256,4096]{1,0:T(8,128)(2,1)} %all-gather.19.cloned.1.call-done) | copy-start | bytes 6291460
  226.3 61.5 %all-to-all-start = ((bf16[4,256,512]{2,1,0:T(8,128)(2,1)}), bf16[4,256,512]{2,1,0:T(8,128)(2,1)S(1)}, u32[]{:S(2)}, u32[]{:S(2)}) async-start(bf16[4,256,512]{2,1,0:T(8,128)(2,1)} %select_convert_fusion), calls=%async_computation | async-start | bytes 2097152 | tf_op jit(solution)/shard_map/all_to_all | solution.py:106
  231.9 5.4 %copy-start.9 = (bf16[1024,2]{0,1:T(2,128)(2,1)S(1)}, bf16[1024,2]{0,1:T(2,128)(2,1)}, u32[]{:S(2)}) copy-start(bf16[1024,2]{0,1:T(2,128)(2,1)} %param.21) | copy-start | bytes 12292
  231.9 57.0 %copy-start.1 = (bf16[1024,1024]{1,0:T(8,128)(2,1)S(1)}, bf16[1024,1024]{1,0:T(8,128)(2,1)}, u32[]{:S(2)}) copy-start(bf16[1024,1024]{1,0:T(8,128)(2,1)} %param.16) | copy-start | bytes 6291460
Sparse Core Ops, SparseCore 0:
  9.9 30.8 all-gather.12
  66.8 28.0 all-gather.14
  120.9 28.0 all-gather.16
  174.2 28.0 all-gather.18
